TPU v7x, 32 devices: a whole 2x2x4 slice. The times are simulated.
32 devices in a mesh: seq: 16 (over z, y, x), fsdp: 2 (over core).
Axes of the slice: x: 2, y: 2, z: 4, core: 2. Of those that a mesh axis runs over, the one named last changes fastest.
Arguments:
- tokens: bfloat16 [2, 12288, 2560], P('fsdp', 'seq'), may hold values from -6 to 6
- bounds: int32 [2, 16, 2], P('fsdp', 'seq'), may hold values from 0 to 24, as said below
- in_weight: bfloat16 [2560, 5416], P(('seq', 'fsdp')), may hold values from -0.125 to 0.125
- conv_weight: float32 [4, 2816], replicated, may hold values from -0.6 to 0.6
- conv_bias: float32 [2816], replicated, may hold values from -3 to 3
- dt_bias: float32 [40], replicated, may hold values from -4 to 0
- decay_rate: float32 [40], replicated, may hold values from 4.8828125e-05 to 0.5
- skip_gain: float32 [40], replicated, may hold values from 0.1 to 1.9
- norm_gain: float32 [2560], replicated, may hold values from 0.1 to 1.9
Outputs:
- layer_out: bfloat16 [2, 12288, 2560], P('fsdp', 'seq')
Inputs may be any that keep to these rules, and one draw needn't show every extreme that they name: For sequence b, bounds[b, s] holds the first and one past the last block of the shard of index s of seq; shards are consecutive in s and cover all 24 blocks; each holds 1 to 3 blocks, and some shard holds 3.
All inputs are finite; a program needn't handle non-finite values.
Results may differ from a plain program's by a relative error of at most 0.0028.
The roundings to bfloat16 on the way count: a program that leaves them out, or rounds other values in their place, can miss the bound.
Values may be sent and summed in bfloat16 or wider, within the bound.
No kernel may reach another device: no remote copies, remote signals or barrier semaphores. Data moves between devices by JAX's collectives and lax.ppermute only.
A program may use at most 192 MiB of HBM per device.

v0:
```python
import jax
import jax.numpy as jnp
from jax import lax
from jax.sharding import PartitionSpec as P

BLOCK = 256


def passed_along(value, axis, steps):
    count = lax.axis_size(axis)
    leading, last = (max(0, -steps), min(count, count - steps))
    return lax.ppermute(value, axis, [(source, source + steps) for source in range(leading, last)])


def carried_in(part, axis, combine, identity):
    place = lax.axis_index(axis)
    gathered = jax.tree.map(lambda a: lax.all_gather(a, axis), part)
    state = jax.tree.map(lambda a, e: jnp.zeros_like(a) + jnp.asarray(e, a.dtype), part, identity)

    def one(turn, state):
        return combine(
            state, jax.tree.map(lambda a: lax.dynamic_index_in_dim(a, turn, 0, False), gathered)
        )

    return lax.fori_loop(0, place, one, state)


def block_terms(head_input, input_map, output_map, step_size, decay_rate):
    log_decay = -(step_size * decay_rate[None, :]).T
    cumulative = jnp.cumsum(log_decay, axis=1)
    pairwise = cumulative[:, :, None] - cumulative[:, None, :]
    length = cumulative.shape[1]
    causal = jnp.arange(length)[:, None] >= jnp.arange(length)[None, :]
    pair_decay = jnp.exp(jnp.where(causal[None], pairwise, -jnp.inf))
    scores = jnp.dot(output_map, input_map.T, preferred_element_type=jnp.float32)
    mixing = scores[None] * pair_decay * step_size.T[:, None, :]
    inner_out = jnp.einsum("hij,jhp->ihp", mixing, head_input, precision=lax.Precision.HIGH)
    to_end = jnp.exp(cumulative[:, -1:] - cumulative) * step_size.T
    local_state = jnp.einsum(
        "hj,jhp,jn->hpn",
        to_end,
        head_input,
        input_map.astype(jnp.float32),
        precision=lax.Precision.HIGH,
    )
    return (inner_out, cumulative, local_state)


def carried(output_map, cumulative, state):
    reach = jnp.einsum(
        "in,hpn->ihp", output_map.astype(jnp.float32), state, precision=lax.Precision.HIGH
    )
    return jnp.exp(cumulative).T[:, :, None] * reach


def compose(earlier, later):
    return (earlier[0] * later[0], later[0][:, None, None] * earlier[1] + later[1])


def local(
    tokens, bounds, in_weight, conv_weight, conv_bias, dt_bias, decay_rate, skip_gain, norm_gain
):
    slots = tokens.shape[1]
    inner = norm_gain.shape[0]
    state_width = (conv_bias.shape[0] - inner) // 2
    heads = decay_rate.shape[0]
    head_dim = inner // heads
    kernel = conv_weight.shape[0]
    capacity = slots // BLOCK
    shard_blocks = bounds[0, 0, 1] - bounds[0, 0, 0]
    own_rows = tokens[0]
    summed = jnp.dot(
        own_rows,
        lax.all_gather(in_weight, ("seq", "fsdp"), axis=0, tiled=True),
        preferred_element_type=jnp.float32,
    )
    projected = summed.astype(jnp.bfloat16)
    gate = projected[:, :inner].astype(jnp.float32)
    mixed_in = projected[:, inner : 2 * inner + 2 * state_width]
    raw_step = projected[:, 2 * inner + 2 * state_width :].astype(jnp.float32)
    edge_rows = lax.dynamic_slice_in_dim(
        mixed_in, shard_blocks * BLOCK - (kernel - 1), kernel - 1, 0
    )
    previous = passed_along(edge_rows, "seq", 1)
    extended = jnp.concatenate([previous, mixed_in], axis=0)
    convolved = jnp.zeros((slots, mixed_in.shape[1]), jnp.float32) + conv_bias[None, :]
    for offset in range(kernel):
        convolved = convolved + conv_weight[offset][None, :] * extended[
            offset : offset + slots
        ].astype(jnp.float32)
    conv_out = jax.nn.silu(convolved).astype(jnp.bfloat16)
    live_mask = jnp.arange(slots)[:, None] < shard_blocks * BLOCK
    step_size = jnp.where(live_mask, jax.nn.softplus(raw_step + dt_bias[None, :]), 0.0)
    pieces = []
    decay_total = jnp.ones((heads,), jnp.float32)
    summary_state = jnp.zeros((heads, head_dim, state_width), jnp.float32)
    for place in range(capacity):
        lower = place * BLOCK
        upper = lower + BLOCK
        in_values = (
            conv_out[lower:upper, :inner].astype(jnp.float32).reshape(BLOCK, heads, head_dim)
        )
        in_map = conv_out[lower:upper, inner : inner + state_width]
        out_map = conv_out[lower:upper, inner + state_width :]
        inner_out, cumulative, local_state = block_terms(
            in_values, in_map, out_map, step_size[lower:upper], decay_rate
        )
        block_decay = jnp.exp(cumulative[:, -1])
        summary_state = block_decay[:, None, None] * summary_state + local_state
        decay_total = decay_total * block_decay
        pieces.append((in_values, out_map, inner_out, cumulative, local_state, block_decay))
    identity = (
        jnp.ones((heads,), jnp.float32),
        jnp.zeros((heads, head_dim, state_width), jnp.float32),
    )
    incoming = carried_in((decay_total, summary_state), "seq", compose, identity)
    state = incoming[1]
    results = []
    for in_values, out_map, inner_out, cumulative, local_state, block_decay in pieces:
        result = (
            inner_out + carried(out_map, cumulative, state) + skip_gain[None, :, None] * in_values
        )
        results.append(result.reshape(BLOCK, inner))
        state = block_decay[:, None, None] * state + local_state
    scanned = jnp.concatenate(results, axis=0)
    gated = scanned * jax.nn.silu(gate)
    normed = (
        gated
        * lax.rsqrt(jnp.mean(gated * gated, axis=1, keepdims=True) + 1e-05)
        * norm_gain[None, :]
    )
    layer_out = jnp.where(live_mask, normed, 0.0).astype(jnp.bfloat16)
    return layer_out[None]


def solution(mesh):
    in_specs = (
        P("fsdp", "seq", None),
        P("fsdp", "seq", None),
        P(("seq", "fsdp"), None),
        P(),
        P(),
        P(),
        P(),
        P(),
        P(),
    )
    out_specs = P("fsdp", "seq", None)
    return jax.shard_map(local, mesh=mesh, in_specs=in_specs, out_specs=out_specs, check_vma=False)
```

profile of v0, /device:TPU:31, one launch (start us, length us, event | category | flops | bytes accessed | tf_op | source)
XLA Modules:
  0.0 540.5 jit_solution(17595913890075685006)
XLA Ops:
  6.5 0.7 all-gather.5.cloned.1.call-update
  7.3 1.4 fusion.94
  10.0 1.1 slice_reduce_fusion.9
  11.0 166.1 %all-gather.5.cloned.1.call-done = bf16[2560,5416]{1,0:T(8,128)(2,1)} async-done(((bf16[80,5416]{1,0:T(8,128)(2,1)}), bf16[2560,5416]{1,0:T(8,128)(2,1)}) %all-gather.5.cloned.1.call-update) | async-done | bytes 27729936 | tf_op jit(solution)/shard_map/all_gather | solution.py:74
  177.1 28.9 %convolution_convert_fusion = bf16[768,5416]{0,1:T(8,128)(2,1)} fusion(bf16[2560,5416]{1,0:T(8,128)(2,1)} %all-gather.5.cloned.1.call-done, bf16[1,768,2560]{2,1,0:T(8,128)(2,1)} %param.11), kind=kOutput, calls=%fused_computation.20 | convolution fusion | flops 21300738048 | bytes 39981056 | tf_op jit(solution)/shard_map/dot_general | solution.py:72
  206.1 4.5 slice.135
  210.6 1.0 fusion.65
  211.6 0.7 slice_bitcast_fusion.2
  212.2 0.6 reduce-window.24
  212.8 0.2 slice_reduce_fusion.1
  213.1 0.6 reduce-window.26
  213.7 0.2 slice_reduce_fusion
  214.0 0.6 reduce-window.20
  214.6 0.2 slice_reduce_fusion.2
  214.9 1.4 constant_dynamic-slice_fusion
  216.3 0.3 copy.36
  216.6 1.5 collective-permute-start
  218.1 0.2 slice_reduce_fusion.3
  218.3 0.8 multiply_bitcast_fusion
  219.1 2.0 collective-permute-done
  221.1 0.4 copy.37
  221.6 15.4 %multiply_convert_fusion = bf16[768,2816]{0,1:T(8,128)(2,1)S(1)} fusion(bf16[768,2816]{0,1:T(8,128)(2,1)} %slice.135, bf16[3,2816]{0,1:T(8,128)(2,1)S(1)} %copy.37, f32[2816]{0:T(1024)S(1)} %get-tuple-element.52, f32[2816]{0:T(1024)S(1)} %get-tuple-element.53, f32[2816]{0:T(1024)S(1)} %get-tuple-element.51, f32[2816]{0:T(1024)S(1)} %get-tuple-element.50, ...), kind=kLoop, calls=%fused_computation.23 | loop fusion | flops 56229888 | bytes 8723968 | tf_op jit(solution)/shard_map/convert_element_type | solution.py:91
  237.0 0.3 fusion.92
  237.3 0.9 fusion.44
  238.2 0.5 copy-done.3
  238.7 0.9 fusion.46
  239.6 0.3 copy-done
  239.9 0.4 copy-done.7
  240.3 0.4 copy-done.1
  240.7 1.9 fusion.56
  242.7 0.6 dynamic-slice
  243.8 0.6 iota_compare_fusion
  244.5 0.2 dynamic-update-slice
  244.7 31.0 %all-reduce = f32[640]{0:T(1024)S(1)} all-reduce(f32[640]{0:T(1024)S(1)} %dynamic-update-slice), channel_id=2, replica_groups=mesh['seq'=16,'fsdp'=2] {'seq'}, use_global_device_ids=true, to_apply=%add | all-reduce | flops 640 | bytes 5120
  275.8 1.1 fusion.84
  276.9 1.1 fusion.77
  278.0 1.1 fusion.74
  279.1 194.9 %all-gather.7.cloned.1.call-done = f32[640,64,128]{2,1,0:T(8,128)} async-done(((f32[40,64,128]{2,1,0:T(8,128)}), f32[640,64,128]{2,1,0:T(8,128)}) %all-gather.7.cloned.1.call-update) | async-done | bytes 20971536 | tf_op jit(solution)/shard_map/all_gather | solution.py:17
  473.9 0.1 broadcast.74
  474.1 24.6 %while.12 = (s32[]{:T(128)}, f32[40,64,128]{2,1,0:T(8,128)S(1)}, s32[]{:T(128)}, f32[16,40]{1,0:T(8,128)S(1)}, f32[16,40,64,128]{3,2,1,0:T(8,128)}, /*index=5*/s32[]{:T(128)}, s32[]{:T(128)}, s32[]{:T(128)}) while((s32[]{:T(128)}, f32[40,64,128]{2,1,0:T(8,128)S(1)}, s32[]{:T(128)}, f32[16,40]{1,0:T(8,128)S(1)}, f32[16,40,64,128]{3,2,1,0:T(8,128)}, ...), condition=%wide.region_7.8_spmd, body=%wide.region_6.7_spmd.sunk | while | flops 655365 | bytes 3932767 | solution.py:25
  474.1 1.6 bitcast_add_fusion.5
  475.8 1.6 bitcast_add_fusion.5
  477.4 1.6 bitcast_add_fusion.5
  479.0 1.6 bitcast_add_fusion.5
  480.6 1.6 bitcast_add_fusion.5
  482.3 1.6 bitcast_add_fusion.5
  483.9 1.6 bitcast_add_fusion.5
  485.5 1.6 bitcast_add_fusion.5
  487.2 1.6 bitcast_add_fusion.5
  488.8 1.6 bitcast_add_fusion.5
  490.4 1.6 bitcast_add_fusion.5
  492.0 1.6 bitcast_add_fusion.5
  493.7 1.6 bitcast_add_fusion.5
  495.3 1.6 bitcast_add_fusion.5
  496.9 1.6 bitcast_add_fusion.5
  498.7 1.8 fusion.71
  500.5 1.7 fusion.64
  502.3 1.8 fusion.57
  504.2 5.2 fusion.45
  509.5 5.5 %fusion.47 = f32[256,40,64]{0,2,1:T(8,128)S(1)} fusion(bf16[256,40,64]{0,2,1:T(8,128)(2,1)S(1)} %bitcast.128, f32[256,40,64]{0,2,1:T(8,128)S(1)} %fusion.64, f32[40,256]{1,0:T(8,128)S(1)} %copy-done.14, f32[40,256]{1,0:T(8,128)S(1)} %copy_bitcast_fusion.1, f32[256,256]{1,0:T(8,128)S(1)} %fusion.77, pred[256,256]{1,0:T(8,128)(4,1)S(1)} %copy-done.9, ...), kind=kOutput, calls=%fused_computation.66 | convolution fusion | flops 1020395520 | bytes 7004320 | tf_op jit(solution)/shard_map/hij,jhp->ihp/dot_general | solution.py:37
  515.0 5.2 fusion.49
  520.2 4.4 multiply_reduce_fusion
  524.7 2.6 fusion.42
  527.3 6.3 %copy.50 = bf16[1,768,2560]{2,1,0:T(8,128)(2,1)} copy(bf16[1,768,2560]{1,2,0:T(8,128)(2,1)} %fusion.42) | data formatting | bytes 7864320 | tf_op jit(solution)/shard_map/broadcast_in_dim | solution.py:133
  (76 shorter events, 0.8 us)
Async XLA Ops:
  6.5 170.6 %all-gather.5.cloned.1.call-start = ((), (), s32[]{:S(2)}) async-start(), calls=%async_computation | async-start | bytes 29061120 | tf_op jit(solution)/shard_map/all_gather | solution.py:74
  7.3 466.7 %all-gather.7.cloned.1.call-start = ((), (), s32[]{:S(2)}) async-start(), calls=%async_computation.1 | async-start | bytes 22282240 | tf_op jit(solution)/shard_map/all_gather | solution.py:17
  206.0 4.5 copy-start.18
  206.1 5.5 %copy-start.19 = (f32[40]{0:T(128)S(1)}, f32[40]{0:T(128)}, u32[]{:S(2)}) copy-start(f32[40]{0:T(128)} %param.17) | copy-start | bytes 484
  210.6 11.0 %copy-start.16 = (f32[2816]{0:T(1024)S(1)}, f32[2816]{0:T(1024)}, u32[]{:S(2)}) copy-start(f32[2816]{0:T(1024)} %param.15) | copy-start | bytes 33796
  216.6 4.5 collective-permute-start
  237.0 2.9 copy-start
  237.3 1.4 copy-start.3
  237.3 2.3 copy-start.5
  237.3 3.0 copy-start.7
  239.6 1.1 copy-start.1
  239.6 3.1 copy-start.21
  498.7 3.5 copy-start.2
  502.3 1.9 copy-start.6
  502.3 1.9 copy-start.9
  502.3 1.9 copy-start.12
  502.3 1.9 copy-start.15
  502.3 1.9 copy-start.20
  504.2 5.3 copy-start.4
  504.2 5.2 copy-start.11
  504.2 5.2 copy-start.14
  509.5 5.5 %copy-start.8 = (bf16[256,2560]{0,1:T(8,128)(2,1)S(1)}, bf16[256,2560]{0,1:T(8,128)(2,1)}, u32[]{:S(2)}) copy-start(bf16[256,2560]{0,1:T(8,128)(2,1)} %copy-done.7) | copy-start | bytes 3932164
  509.5 5.5 %copy-start.10 = (f32[256,40]{0,1:T(8,128)S(1)}, f32[256,40]{0,1:T(8,128)}, u32[]{:S(2)}) copy-start(f32[256,40]{0,1:T(8,128)} %get-tuple-element.87) | copy-start | bytes 122884
  509.5 5.5 %copy-start.13 = (f32[40,256]{1,0:T(8,128)S(1)}, f32[40,256]{1,0:T(8,128)}, u32[]{:S(2)}) copy-start(f32[40,256]{1,0:T(8,128)} %get-tuple-element.78) | copy-start | bytes 122884
  520.2 4.5 copy-start.17
Sparse Core Ops, SparseCore 0:
  10.2 166.9 all-gather.4
  242.8 231.1 all-gather.6
where the time goes:
time: 542 us; the launch traced here: 540 us
  waiting for transfers between devices  364 us (67%)
  matrix products  57 us (11%)
  other arithmetic  51.6 us (10%)
  blocking collectives  31 us (6%)
  local copies, waits for them, and re-layouts  18.9 us (3%)
  between operations  15.7 us (3%)
    all_gather x1, waiting for transfers between devices, carried_in(): gathered = jax.tree.map(lambda a: lax.all_gather(a, axis), part)  195 us
    all_gather x1, waiting for transfers between devices, local(): lax.all_gather(in_weight, ('seq', 'fsdp'), axis=0, tiled=True)  166 us
    unnamed x1, blocking collectives  31 us
    dot_general x1, matrix products, local(): jnp.dot(own_rows, lax.all_gather(in_weight, ('seq', 'fsdp'), axis=0, tile...  28.9 us
    add x15, other arithmetic, compose(): later[0][:, None, None] * earlier[1] + later[1]  23.7 us
    dot_general x3, matrix products, block_terms(): jnp.einsum('hij,jhp->ihp', mixing, head_input, precision=lax.Precision.HIGH)  15.9 us
    convert_element_type x1, other arithmetic, local(): conv_out = jax.nn.silu(convolved).astype(jnp.bfloat16)  15.4 us
  transfers between devices with their start and end apart: 3, of which 3 were waited for; matrix products, arithmetic and copies ran while one was open for 2% of the time, Pallas kernels for 0%

commit v1 on v0

v1 whole, which is shorter than its diff:
```python
import functools

import jax
import jax.numpy as jnp
import numpy as np
from jax import lax
from jax.experimental import pallas as pl
from jax.experimental.pallas import tpu as pltpu
from jax.sharding import PartitionSpec as P


BLOCK = 256
TILE = 256
LANES = 128
HALO = 16
AXES = ("seq", "fsdp")
LOG2E = 1.4426950408889634
VMEM = pltpu.VMEM
F32 = jnp.float32
BF16 = jnp.bfloat16


def split2(f):
    hi = f.astype(BF16)
    return hi, (f - hi.astype(F32)).astype(BF16)


def split3(f):
    hi = f.astype(BF16)
    rest = f - hi.astype(F32)
    mid = rest.astype(BF16)
    return hi, mid, (rest - mid.astype(F32)).astype(BF16)


def dot(a, b):
    return jnp.dot(a, b, preferred_element_type=F32)


def dot_rows(a, b):
    return lax.dot_general(a, b, (((0,), (0,)), ((), ())), preferred_element_type=F32)


def packed(f, heads):
    lane = lax.broadcasted_iota(jnp.int32, f.shape, 1)
    keep = lambda v: jnp.where(lane < heads, v, 0.0)
    hi = f.astype(BF16).astype(F32)
    mid = (f - hi).astype(BF16).astype(F32)
    lo = f - hi - mid
    return (keep(hi) + pltpu.roll(keep(mid), heads, 1) + pltpu.roll(keep(lo), 2 * heads, 1)).astype(BF16)


def expander(width, first_head, head_dim, heads):
    row = lax.broadcasted_iota(jnp.int32, (LANES, width), 0)
    lane = lax.broadcasted_iota(jnp.int32, (LANES, width), 1)
    head = row - jnp.where(row >= 2 * heads, 2 * heads, jnp.where(row >= heads, heads, 0))
    low = (head - first_head) * head_dim
    return jnp.where((lane >= low) & (lane < low + head_dim) & (row < 3 * heads), 1.0, 0.0).astype(BF16)


def silu(a):
    return a * (1.0 / (1.0 + jnp.exp(-a)))


def weight_copies(pieces, offsets_ref, weight, sem, rows, low, high):
    copies = []
    number = 0
    for piece in pieces:
        for part in range(piece.shape[0] // rows):
            to = pl.multiple_of(offsets_ref[number], 16)
            at = pl.ds(low, high - low)
            copies.append(
                pltpu.make_async_copy(
                    piece.at[pl.ds(part * rows, rows), at], weight.at[pl.ds(to, rows), at], sem
                )
            )
            number += 1
    return copies


def begin(copies):
    for copy in copies:
        copy.start()


def finish(copies):
    for copy in copies:
        copy.wait()


def project_kernel(count, rows, base, extra, has_step, *refs):
    offsets_ref, blocks_ref = refs[:2]
    pieces = refs[2 : 2 + count]
    refs = refs[2 + count :]
    if has_step:
        tokens, halo, taps, bias, scalars = refs[:5]
        out, step_out, cum_out, ext, weight, acc, sem = refs[5:]
    else:
        tokens, halo, taps, bias = refs[:4]
        out, ext, weight, acc, sem = refs[4:]
    slots = tokens.shape[0]
    width = weight.shape[1]
    tiles = out.shape[1] // TILE
    plain = tiles - (1 if has_step else 0)
    first_tiles = 2
    cut = first_tiles * TILE
    inputs = [
        pltpu.make_async_copy(halo, ext.at[pl.ds(0, HALO), :], sem.at[0]),
        pltpu.make_async_copy(tokens, ext.at[pl.ds(HALO, slots), :], sem.at[0]),
    ]
    inputs += weight_copies(pieces, offsets_ref, weight, sem.at[0], rows, 0, cut)
    others = weight_copies(pieces, offsets_ref, weight, sem.at[1], rows, cut, width)
    begin(inputs)
    begin(others)
    finish(inputs)
    kernel = taps.shape[0]

    def epilogue(t, slot):
        column = jnp.where(t < plain, base + t * TILE, extra)
        from_ = pl.ds(pl.multiple_of(column, LANES), TILE)
        at = pl.ds(pl.multiple_of(t * TILE, TILE), TILE)
        tap = taps[:, from_]
        start = bias[:, from_]
        for block in range(slots // BLOCK):
            total = start + jnp.zeros((BLOCK, TILE), F32)
            for k in range(kernel):
                first = HALO - (kernel - 1) + k + block * BLOCK
                total = total + tap[k : k + 1, :] * acc[slot, first : first + BLOCK, :]
            out[block * BLOCK : (block + 1) * BLOCK, at] = silu(total).astype(BF16)

    def tile(t, carry):
        epilogue(jnp.maximum(t - 1, 0), lax.rem(t + 1, 2))
        at = pl.ds(pl.multiple_of(t * TILE, TILE), TILE)
        acc[lax.rem(t, 2)] = dot(ext[...], weight[:, at]).astype(BF16).astype(F32)
        return carry

    lax.fori_loop(0, first_tiles, tile, 0)
    finish(others)
    lax.fori_loop(first_tiles, tiles, tile, 0)
    if has_step:
        first = tiles * TILE
        raw_all = dot(ext[HALO:, :], weight[:, first : first + LANES]).astype(BF16).astype(F32)
        row = lax.broadcasted_iota(jnp.int32, (BLOCK, BLOCK), 0)
        col = lax.broadcasted_iota(jnp.int32, (BLOCK, BLOCK), 1)
        lower = jnp.where(row >= col, 1.0, 0.0).astype(BF16)
        token = lax.broadcasted_iota(jnp.int32, (BLOCK, LANES), 0)
        for block in range(slots // BLOCK):
            low, high = block * BLOCK, (block + 1) * BLOCK
            a = raw_all[low:high] + scalars[0:1, :]
            size = jnp.maximum(a, 0.0) + jnp.log1p(jnp.exp(-jnp.abs(a)))
            size = jnp.where(token + low < blocks_ref[0] * BLOCK, size, 0.0)
            hi, mid, lo = split3(-(size * scalars[1:2, :]))
            step_out[low:high, :] = size
            cum_out[low:high, :] = dot(lower, hi) + dot(lower, mid) + dot(lower, lo)
    epilogue(tiles - 1, (tiles - 1) % 2)


def summary_kernel(first_head, head_dim, heads, x_ref, bc_ref, cum_ref, step_ref, starts, summary, state, total):
    width = x_ref.shape[1]
    state_width = bc_ref.shape[1] // 2
    block = pl.program_id(0)

    @pl.when(block == 0)
    def _():
        state[...] = jnp.zeros_like(state)
        total[...] = jnp.ones_like(total)

    onehot = expander(width, first_head, head_dim, heads)
    cum = cum_ref[...]
    last = cum[BLOCK - 1 : BLOCK, :]
    to_end = dot(packed(jnp.exp(last - cum) * step_ref[...], heads), onehot)
    hi, lo = split2(x_ref[...].astype(F32) * to_end)
    b = bc_ref[:, :state_width]
    local = dot_rows(b, hi) + dot_rows(b, lo)
    decay = dot(packed(jnp.exp(last) + jnp.zeros((8, LANES), F32), heads), onehot)
    starts[0] = state[...]
    state[...] = decay[:1, :] * state[...] + local
    total[...] = total[...] * decay

    @pl.when(block == pl.num_programs(0) - 1)
    def _():
        quarter = summary.shape[2]
        for q in range(summary.shape[0]):
            summary[q, :state_width, :] = state[:, q * quarter : (q + 1) * quarter]
            summary[q, state_width:, :] = total[:, q * quarter : (q + 1) * quarter]


def inner_kernel(first_head, head_dim, heads, x_ref, bc_ref, cum_ref, step_ref, scalars, starts, y_ref):
    width = x_ref.shape[1]
    state_width = bc_ref.shape[1] // 2
    half = BLOCK // 2
    b = bc_ref[:, :state_width]
    c = bc_ref[:, state_width:]
    scores = lax.dot_general(c, b, (((1,), (1,)), ((), ())), preferred_element_type=F32)
    cum = cum_ref[...]
    step = step_ref[...]
    scaled = cum * LOG2E
    log_step = jnp.where(step > 0.0, jnp.log(step) * LOG2E, -1e30)
    across = (log_step - scaled).T
    onehot = expander(width, first_head, head_dim, heads)
    reach_decay = dot(packed(jnp.exp(cum), heads), onehot)
    skip = dot(packed(scalars[2:3, :] + jnp.zeros((8, LANES), F32), heads), onehot)
    row = lax.broadcasted_iota(jnp.int32, (half, half), 0)
    col = lax.broadcasted_iota(jnp.int32, (half, half), 1)
    causal = row >= col
    lane = lax.broadcasted_iota(jnp.int32, (1, LANES), 1)
    per = LANES // head_dim
    cc = jnp.concatenate([c, c], axis=1)
    for group in range(width // LANES):
        at = slice(group * LANES, (group + 1) * LANES)
        x = x_ref[:, at]
        reach = dot(cc, jnp.concatenate(split2(starts[0, :, at]), axis=0))
        base = reach * reach_decay[:, at] + skip[:1, at] * x.astype(F32)
        top, low = base[:half], base[half:]
        for member in range(per):
            head = first_head + group * per + member
            mine = (lane >= member * head_dim) & (lane < (member + 1) * head_dim)
            own = jnp.where(mine, x, jnp.zeros_like(x))
            down = scaled[:, head : head + 1]
            right = across[head : head + 1, :]
            m00 = jnp.where(causal, jnp.exp2(down[:half] + right[:, :half]) * scores[:half, :half], 0.0)
            m10 = jnp.exp2(down[half:] + right[:, :half]) * scores[half:, :half]
            m11 = jnp.where(causal, jnp.exp2(down[half:] + right[:, half:]) * scores[half:, half:], 0.0)
            hi, lo = split2(m00)
            top = top + (dot(hi, own[:half]) + dot(lo, own[:half]))
            hi, lo = split2(jnp.concatenate([m10, m11], axis=1))
            low = low + (dot(hi, own) + dot(lo, own))
        y_ref[:half, at] = top
        y_ref[half:, at] = low


def gate_kernel(count, rows, *refs):
    offsets_ref = refs[0]
    pieces = refs[1 : 1 + count]
    tokens_hbm, out, tokens, weight, sem = refs[1 + count :]
    width = weight.shape[1]
    inputs = [pltpu.make_async_copy(tokens_hbm, tokens, sem.at[0])]
    inputs += weight_copies(pieces, offsets_ref, weight, sem.at[0], rows, 0, TILE)
    others = weight_copies(pieces, offsets_ref, weight, sem.at[1], rows, TILE, width)
    begin(inputs)
    begin(others)
    finish(inputs)

    def tile(t, carry):
        at = pl.ds(pl.multiple_of(t * TILE, TILE), TILE)
        out[:, at] = dot(tokens[...], weight[:, at]).astype(BF16)
        return carry

    tile(0, 0)
    finish(others)
    lax.fori_loop(1, width // TILE, tile, 0)


def final_kernel(head_dim, heads, blocks_ref, *refs):
    gates, ys, states = refs[:2], refs[2:4], refs[4:6]
    bc_ref, cum_ref, gain, out, earlier, gated = refs[6:]
    state_width = bc_ref.shape[1] // 2
    whole = out.shape[1]
    block = pl.program_id(0)

    @pl.when(block == 0)
    def _():
        earlier[...] = jnp.zeros_like(earlier)

    def part(pair, column):
        first = pair[0].shape[1]
        ref, low = (pair[0], column) if column < first else (pair[1], column - first)
        return ref[:, low : low + TILE]

    cum = cum_ref[...]
    factors = packed(jnp.exp(cum + earlier[:1, :]), heads)
    earlier[...] = earlier[...] + cum[BLOCK - 1 : BLOCK, :]
    c = bc_ref[:, state_width:]
    twice = jnp.concatenate([c, c], axis=1)
    squares = jnp.zeros((BLOCK, LANES), F32)
    for column in range(0, whole, TILE):
        both = jnp.concatenate(split2(part(states, column)), axis=0)
        reach = dot(twice, both)
        decay = dot(factors, expander(TILE, column // head_dim, head_dim, heads))
        value = (part(ys, column) + decay * reach) * silu(part(gates, column).astype(F32))
        gated[:, column : column + TILE] = value
        square = value * value
        for lane in range(0, TILE, LANES):
            squares = squares + square[:, lane : lane + LANES]
    scale = lax.rsqrt(jnp.sum(squares, axis=1, keepdims=True) / whole + 1e-05)
    live = block < blocks_ref[0]
    for column in range(0, whole, TILE):
        at = slice(column, column + TILE)
        out[:, at] = jnp.where(live, gated[:, at] * scale * gain[:, at], 0.0).astype(BF16)


HBM = pl.BlockSpec(memory_space=pltpu.HBM)
FULL = pl.BlockSpec(memory_space=pltpu.VMEM)
SCALARS = pl.BlockSpec(memory_space=pltpu.SMEM)
MIB = 1024 * 1024


def like(shape, dtype):
    return jax.ShapeDtypeStruct(shape, dtype)


def call(kernel, in_specs, out_shape, scratch, flops, limit, *args):
    return pl.pallas_call(
        kernel,
        in_specs=in_specs,
        out_specs=jax.tree.map(lambda _: FULL, out_shape),
        out_shape=out_shape,
        scratch_shapes=scratch,
        cost_estimate=pl.CostEstimate(flops=flops, bytes_accessed=16_000_000, transcendentals=0),
        compiler_params=pltpu.CompilerParams(vmem_limit_bytes=limit * MIB),
    )(*args)


def project(pieces, rows, offsets, blocks, tokens, halo, taps, bias, base, extra, scalars):
    slots, depth = tokens.shape
    width = pieces[0].shape[1]
    has_step = scalars is not None
    conv = width - LANES if has_step else width
    out = [like((slots, conv), BF16)]
    if has_step:
        out += [like((slots, LANES), F32)] * 2
    return call(
        functools.partial(project_kernel, len(pieces), rows, base, extra, has_step),
        [SCALARS] * 2 + [HBM] * (len(pieces) + 2) + [FULL] * (3 if has_step else 2),
        out,
        [
            VMEM((slots + HALO, depth), BF16),
            VMEM((depth, width), BF16),
            VMEM((2, slots + HALO, TILE), F32),
            pltpu.SemaphoreType.DMA((2,)),
        ],
        2 * slots * depth * width, 40,
        offsets, blocks, *pieces, tokens, halo, taps, bias, *([scalars] if has_step else []),
    )


def by_block(width, column=0):
    return pl.BlockSpec((BLOCK, width), lambda i: (i, column))


def summarize(x, width, first, bc_at, state_width, cum, step, first_head, head_dim, heads, parts):
    slots = x.shape[0]
    count = slots // BLOCK
    shape = (parts, state_width + 8, width // parts)
    return pl.pallas_call(
        functools.partial(summary_kernel, first_head, head_dim, heads),
        name="summary",
        grid=(count,),
        in_specs=[by_block(width), by_block(2 * state_width, bc_at), by_block(LANES), by_block(LANES)],
        out_specs=[
            pl.BlockSpec((1, state_width, width), lambda i: (i, 0, 0)),
            pl.BlockSpec(shape, lambda i: (0, 0, 0)),
        ],
        out_shape=[like((count, state_width, width), F32), like(shape, F32)],
        scratch_shapes=[VMEM((state_width, width), F32), VMEM((8, width), F32)],
        cost_estimate=pl.CostEstimate(flops=4 * slots * state_width * width, bytes_accessed=8_000_000, transcendentals=0),
        compiler_params=pltpu.CompilerParams(vmem_limit_bytes=40 * MIB),
    )(x, first, cum, step)


def inner(x, width, first, bc_at, state_width, cum, step, scalars, starts, first_head, head_dim, heads):
    slots = x.shape[0]
    return pl.pallas_call(
        functools.partial(inner_kernel, first_head, head_dim, heads),
        name="inner",
        grid=(slots // BLOCK,),
        in_specs=[
            by_block(width), by_block(2 * state_width, bc_at), by_block(LANES), by_block(LANES),
            pl.BlockSpec((8, LANES), lambda i: (0, 0)),
            pl.BlockSpec((1, state_width, width), lambda i: (i, 0, 0)),
        ],
        out_specs=by_block(width),
        out_shape=like((slots, width), F32),
        cost_estimate=pl.CostEstimate(flops=6 * slots * BLOCK * width, bytes_accessed=8_000_000, transcendentals=0),
        compiler_params=pltpu.CompilerParams(vmem_limit_bytes=40 * MIB),
    )(x, first, cum, step, scalars, starts)


def gate_columns(pieces, rows, offsets, tokens):
    slots, depth = tokens.shape
    width = pieces[0].shape[1]
    return call(
        functools.partial(gate_kernel, len(pieces), rows),
        [SCALARS] + [HBM] * (len(pieces) + 1),
        like((slots, width), BF16),
        [VMEM((slots, depth), BF16), VMEM((depth, width), BF16), pltpu.SemaphoreType.DMA((2,))],
        2 * slots * depth * width, 32,
        offsets, *pieces, tokens,
    )


def finished(blocks, gates, ys, states, first, bc_at, state_width, cum, gain, head_dim, heads):
    slots = cum.shape[0]
    whole = gain.shape[1]
    full = lambda a: pl.BlockSpec(a.shape, lambda i: (0, 0))
    return pl.pallas_call(
        functools.partial(final_kernel, head_dim, heads),
        name="final",
        grid=(slots // BLOCK,),
        in_specs=[SCALARS] + [by_block(a.shape[1]) for a in gates + ys] + [full(a) for a in states]
        + [by_block(2 * state_width, bc_at), by_block(LANES), full(gain)],
        out_specs=by_block(whole),
        out_shape=like((slots, whole), BF16),
        scratch_shapes=[VMEM((8, LANES), F32), VMEM((BLOCK, whole), F32)],
        cost_estimate=pl.CostEstimate(flops=8 * slots * state_width * whole, bytes_accessed=16_000_000, transcendentals=0),
        compiler_params=pltpu.CompilerParams(vmem_limit_bytes=40 * MIB),
    )(blocks, *gates, *ys, *states, first, cum, gain)


PLANE = 4


def routes(planes, cores):
    ids = lambda z, m, c: (z * PLANE + m) * cores + c
    places = [(z, m, c) for z in range(planes) for m in range(PLANE) for c in range(cores)]
    beside = lambda turn: [(ids(z, m, c), ids(z, m ^ (1 if c % 2 == turn else 2), c)) for z, m, c in places]
    return dict(
        long=[[(ids(z, m, c), ids((z + k) % planes, m, c)) for z, m, c in places] for k in range(planes)],
        beside=[beside(0), beside(1)],
        swap=[(ids(z, m, c), ids(z, m, cores - 1 - c)) for z, m, c in places],
        cross=[[(ids(z, m, c), ids(z, m ^ a, c)) for z, m, c in places] for a in range(PLANE)],
        later=[[(ids(z, m, c), ids(z + k, m, c)) for z, m, c in places if z + k < planes] for k in range(planes)],
        after=[(s, s + cores) for s in range((planes * PLANE - 1) * cores)],
    )


def send(value, pairs):
    return lax.ppermute(value, AXES, pairs)


def moved(held, pairs):
    value, blocks = held
    landed = np.zeros_like(blocks)
    for source, target in pairs:
        landed[target] = blocks[source]
    return send(value, pairs), landed


def joined(parts):
    return jnp.concatenate([v for v, _ in parts], axis=0), np.concatenate([b for _, b in parts], axis=1)


def along(held, paths, planes):
    return [held] + [moved(held, paths["long"][k]) for k in range(1, planes)]


def around(held, paths):
    near = moved(held, paths["beside"][0])
    side = moved(held, paths["beside"][1])
    return [held, near, side, moved(near, paths["beside"][1])]


def collect(chunk, paths, planes, cores, rows, place, long_first):
    if rows % HALO or planes > PLANE:
        return [lax.all_gather(chunk, AXES, axis=0, tiled=True)], jnp.zeros((1,), jnp.int32), rows * planes * PLANE * cores
    own = (chunk, np.arange(planes * PLANE * cores)[:, None])
    if long_first:
        line = around(joined(along(own, paths, planes)), paths)
    else:
        line = along(joined(around(own, paths)), paths, planes)
    line = line + [moved(held, paths["swap"]) for held in line]
    table = np.concatenate([b for _, b in line], axis=1) * rows
    return [v for v, _ in line], jnp.asarray(table, jnp.int32)[place], rows


def compose(earlier, later, wide):
    decay = later[wide:]
    return jnp.concatenate([decay[:1] * earlier[:wide] + later[:wide], earlier[wide:] * decay], axis=0)


def pick(parts, index):
    return lax.dynamic_index_in_dim(parts, index, 0, False)


def carried_in(summary, paths, planes, mine, wide):
    parts = jnp.stack(
        [pick(summary, mine)]
        + [send(pick(summary, mine ^ a), paths["cross"][a]) for a in range(1, PLANE)]
    )
    members = [pick(parts, mine ^ m) for m in range(PLANE)]
    totals = [members[0]]
    for member in members[1:]:
        totals.append(compose(totals[-1], member, wide))
    state = jnp.zeros_like(summary[0, :wide])
    for k in range(planes - 1, 0, -1):
        part = send(totals[-1], paths["later"][k])
        state = part[wide : wide + 1] * state + part[:wide]
    states = jnp.stack([state] + [t[wide : wide + 1] * state + t[:wide] for t in totals[:-1]])
    back = jnp.stack([pick(states, mine)] + [send(pick(states, mine ^ a), paths["cross"][a]) for a in range(1, PLANE)])
    return jnp.concatenate([pick(back, mine ^ q) for q in range(PLANE)], axis=1)


def local(tokens, bounds, in_weight, conv_weight, conv_bias, dt_bias, decay_rate, skip_gain, norm_gain):
    cores = lax.axis_size("fsdp")
    planes = lax.axis_size("seq") // PLANE
    place = lax.axis_index("seq") * cores + lax.axis_index("fsdp")
    mine = lax.axis_index("seq") % PLANE
    paths = routes(planes, cores)
    own = tokens[0]
    rows = in_weight.shape[0]
    inner_width = norm_gain.shape[0]
    state_width = (conv_bias.shape[0] - inner_width) // 2
    heads = decay_rate.shape[0]
    head_dim = inner_width // heads
    early = heads * 2 // 5 // 8 * 8
    cut = early * head_dim
    live = bounds[0, 0, 1] - bounds[0, 0, 0]
    blocks = live[None]
    scalars = jnp.pad(jnp.stack([dt_bias, decay_rate, skip_gain]), ((0, 5), (0, LANES - heads)))

    rest = jnp.pad(in_weight[:, 2 * inner_width :], ((0, 0), (0, LANES - heads)))
    chunks = [
        jnp.concatenate([in_weight[:, inner_width : inner_width + cut], rest], axis=1),
        in_weight[:, inner_width + cut : 2 * inner_width],
        in_weight[:, : inner_width - cut],
        in_weight[:, inner_width - cut : inner_width],
    ]
    edge = lax.dynamic_slice_in_dim(own, live * BLOCK - HALO, HALO, 0)
    halo = send(edge, paths["after"])
    weights = [collect(chunk, paths, planes, cores, rows, place, i < LONG_FIRST) for i, chunk in enumerate(chunks)]

    bias = conv_bias[None]
    first, step, cum = project(
        weights[0][0], weights[0][2], weights[0][1], blocks, own, halo, conv_weight, bias, 0, inner_width, scalars
    )
    (second,) = project(
        weights[1][0], weights[1][2], weights[1][1], blocks, own, halo, conv_weight, bias, cut, cut, None
    )
    x = [first, second]
    widths = [cut, inner_width - cut]
    firsts = [0, early]
    bc_at = cut // (2 * state_width)
    parts, states, ys = [], [], []
    for i in range(2):
        parts.append(
            summarize(x[i], widths[i], first, bc_at, state_width, cum, step, firsts[i], head_dim, heads, PLANE)
        )
    for i in range(2):
        states.append(carried_in(parts[i][1], paths, planes, mine, state_width))
    for i in range(2):
        ys.append(
            inner(x[i], widths[i], first, bc_at, state_width, cum, step, scalars, parts[i][0], firsts[i], head_dim, heads)
        )
    gates = []
    for i in range(2):
        gates.append(gate_columns(weights[2 + i][0], weights[2 + i][2], weights[2 + i][1], own))
    out = finished(blocks, gates, ys, states, first, bc_at, state_width, cum, norm_gain[None], head_dim, heads)
    return out[None]


LONG_FIRST = 3


def solution(mesh):
    whole = P("fsdp", "seq", None)
    in_specs = (whole, whole, P(("seq", "fsdp"), None)) + (P(),) * 6

    return jax.shard_map(local, mesh=mesh, in_specs=in_specs, out_specs=whole, check_vma=False)
```

time: 542 us -> 335 us (0.62)
  the two profiles are of different devices: /device:TPU:31 before, /device:TPU:16 now
where the time goes in v1:
time: 335 us; the launch traced here: 334 us
  waiting for transfers between devices  153 us (46%)
  Pallas kernels  73.3 us (22%)
  starting transfers between devices  57.3 us (17%)
  local copies, waits for them, and re-layouts  41.1 us (12%)
  other arithmetic  7.43 us (2%)
    ppermute x59, waiting for transfers between devices, send(): return lax.ppermute(value, AXES, pairs)  153 us
    ppermute x59, starting transfers between devices, send(): return lax.ppermute(value, AXES, pairs)  57.3 us
    pallas_call x4, Pallas kernels, call(): pl.pallas_call(kernel, in_specs=in_specs, out_specs=jax.tree.map(lambda _...  43.5 us
    unnamed x104, local copies, waits for them, and re-layouts  32.9 us
    pallas_call x2, Pallas kernels, inner(): pl.pallas_call(functools.partial(inner_kernel, first_head, head_dim, head...  15.4 us
    pallas_call x1, Pallas kernels, finished(): pl.pallas_call(functools.partial(final_kernel, head_dim, heads), name='fi...  8.35 us
  transfers between devices with their start and end apart: 59, of which 18 were waited for; matrix products, arithmetic and copies ran while one was open for 4% of the time, Pallas kernels for 19%

profile of v1, /device:TPU:16, one launch (start us, length us, event | category | flops | bytes accessed | tf_op | source)
XLA Modules:
  0.0 334.2 jit_solution(6332967159299313390)
XLA Ops:
  1.0 1.6 collective-permute-start.11
  2.6 1.5 collective-permute-start.10
  5.5 3.5 %collective-permute-start.21 = (bf16[80,1408]{1,0:T(8,128)(2,1)S(1)}, bf16[80,1408]{1,0:T(8,128)(2,1)S(1)}, u32[]{:S(2)}, u32[]{:S(2)}) collective-permute-start(bf16[80,1408]{1,0:T(8,128)(2,1)S(1)} %pad_maximum_fusion.12), channel_id=1, source_target_pairs={{0,16},{1,17},{2,18},{3,19},{4,20},{5,21},{6,22},{7,23},{8,24},{9,... | collective-permute-start | bytes 675848 | tf_op jit(solution)/shard_map/ppermute | solution.py:427
  9.0 1.1 fusion.31
  12.0 7.4 %collective-permute-done.22 = bf16[80,1408]{1,0:T(8,128)(2,1)S(1)} collective-permute-done((bf16[80,1408]{1,0:T(8,128)(2,1)S(1)}, bf16[80,1408]{1,0:T(8,128)(2,1)S(1)}, u32[]{:S(2)}, u32[]{:S(2)}) %collective-permute-start.22) | collective-permute-done | bytes 225312 | tf_op jit(solution)/shard_map/ppermute | solution.py:427
  19.4 3.0 collective-permute-start.33
  22.3 3.5 %collective-permute-done.21 = bf16[80,1408]{1,0:T(8,128)(2,1)S(1)} collective-permute-done((bf16[80,1408]{1,0:T(8,128)(2,1)S(1)}, bf16[80,1408]{1,0:T(8,128)(2,1)S(1)}, u32[]{:S(2)}, u32[]{:S(2)}) %collective-permute-start.21) | collective-permute-done | bytes 225312 | tf_op jit(solution)/shard_map/ppermute | solution.py:427
  25.8 6.9 %collective-permute-done.20 = bf16[80,1408]{1,0:T(8,128)(2,1)S(1)} collective-permute-done((bf16[80,1408]{1,0:T(8,128)(2,1)S(1)}, bf16[80,1408]{1,0:T(8,128)(2,1)S(1)}, u32[]{:S(2)}, u32[]{:S(2)}) %collective-permute-start.20) | collective-permute-done | bytes 225312 | tf_op jit(solution)/shard_map/ppermute | solution.py:427
  34.4 3.4 %collective-permute-start.30 = (bf16[16,2560]{1,0:T(8,128)(2,1)S(1)}, bf16[16,2560]{1,0:T(8,128)(2,1)S(1)}, u32[]{:S(2)}, u32[]{:S(2)}) collective-permute-start(bf16[16,2560]{1,0:T(8,128)(2,1)S(1)} %dynamic-slice_bitcast_fusion.28), channel_id=1, source_target_pairs={{0,2},{1,3},{2,4},{3,5},{4,6},{5,7},{6,8},{7,9},{8,10},{9,11},{10,... | collective-permute-start | bytes 245768 | tf_op jit(solution)/shard_map/ppermute | solution.py:427
  38.4 9.4 %collective-permute-done.30.refs_11_ = bf16[16,2560]{1,0:T(8,128)(2,1)S(1)} collective-permute-done((bf16[16,2560]{1,0:T(8,128)(2,1)S(1)}, bf16[16,2560]{1,0:T(8,128)(2,1)S(1)}, u32[]{:S(2)}, u32[]{:S(2)}) %collective-permute-start.30) | collective-permute-done | bytes 81952 | tf_op jit(solution)/shard_map/ppermute | solution.py:427
  49.8 4.7 %collective-permute-start.1 = (bf16[80,1536]{1,0:T(8,128)(2,1)S(1)}, bf16[80,1536]{1,0:T(8,128)(2,1)S(1)}, u32[]{:S(2)}, u32[]{:S(2)}) collective-permute-start(bf16[80,1536]{1,0:T(8,128)(2,1)S(1)} %get-tuple-element.38), channel_id=1, source_target_pairs={{0,16},{1,17},{2,18},{3,19},{4,20},{5,21},{6,22},{7,23},{8,24},{9,... | collective-permute-start | bytes 737288 | tf_op jit(solution)/shard_map/ppermute | solution.py:427
  54.6 1.1 pad_maximum_fusion.7.refs_1_
  55.7 8.9 %collective-permute-done.32 = bf16[80,1536]{1,0:T(8,128)(2,1)S(1)} collective-permute-done((bf16[80,1536]{1,0:T(8,128)(2,1)S(1)}, bf16[80,1536]{1,0:T(8,128)(2,1)S(1)}, u32[]{:S(2)}, u32[]{:S(2)}) %collective-permute-start.32) | collective-permute-done | bytes 245792 | tf_op jit(solution)/shard_map/ppermute | solution.py:427
  64.6 7.4 %collective-permute-done.31 = bf16[80,1536]{1,0:T(8,128)(2,1)S(1)} collective-permute-done((bf16[80,1536]{1,0:T(8,128)(2,1)S(1)}, bf16[80,1536]{1,0:T(8,128)(2,1)S(1)}, u32[]{:S(2)}, u32[]{:S(2)}) %collective-permute-start.31) | collective-permute-done | bytes 245792 | tf_op jit(solution)/shard_map/ppermute | solution.py:427
  72.1 2.0 collective-permute-start
  75.1 2.1 collective-permute-start.24
  77.2 15.6 %collective-permute-done = bf16[80,1536]{1,0:T(8,128)(2,1)S(1)} collective-permute-done((bf16[80,1536]{1,0:T(8,128)(2,1)S(1)}, bf16[80,1536]{1,0:T(8,128)(2,1)S(1)}, u32[]{:S(2)}, u32[]{:S(2)}) %collective-permute-start) | collective-permute-done | bytes 245792 | tf_op jit(solution)/shard_map/ppermute | solution.py:427
  95.0 1.5 collective-permute-start.13
  97.6 36.4 %collective-permute-done.14.refs_3_ = bf16[320,1024]{1,0:T(8,128)(2,1)S(1)} collective-permute-done((bf16[320,1024]{1,0:T(8,128)(2,1)S(1)}, bf16[320,1024]{1,0:T(8,128)(2,1)S(1)}, u32[]{:S(2)}, u32[]{:S(2)}) %collective-permute-start.14) | collective-permute-done | bytes 655392 | tf_op jit(solution)/shard_map/ppermute | solution.py:427
  134.1 1.1 collective-permute-done.13.refs_2_
  136.7 1.7 collective-permute-start.35
  138.5 18.5 %collective-permute-done.34.refs_3_ = bf16[320,1536]{1,0:T(8,128)(2,1)} collective-permute-done((bf16[320,1536]{1,0:T(8,128)(2,1)}, bf16[320,1536]{1,0:T(8,128)(2,1)}, u32[]{:S(2)}, u32[]{:S(2)}) %collective-permute-start.34) | collective-permute-done | bytes 983072 | tf_op jit(solution)/shard_map/ppermute | solution.py:427
  159.0 2.3 pad_maximum_fusion.refs_1_
  161.8 2.1 copy-done.9
  163.9 1.2 copy-done.20
  165.9 14.3 %shard_map.129 = (bf16[768,1280]{1,0:T(8,128)(2,1)S(1)}, f32[768,128]{1,0:T(8,128)S(1)}, f32[768,128]{1,0:T(8,128)S(1)}) custom-call(s32[32]{0:T(128)S(1)} %get-tuple-element.75.refs_0_, s32[1]{0:T(128)} %bitcast.refs_1_.blocks_ref, bf16[320,1408]{1,0:T(8,128)(2,1)S(1)} %copy-done.8, bf16[320,1408]{1,0:T(8,128)(2,1)S(1)} %copy-done.20, ...), custom_call_target="tpu_custom_call" | custom-call | flops 5536481280 | bytes 16000000 | tf_op jit(solution)/shard_map/pallas_call | solution.py:302
  180.2 2.6 summary.2
  182.8 1.1 copy-done.5
  186.3 2.2 collective-permute-start.43
  190.7 13.1 %collective-permute-done.43 = f32[136,256]{1,0:T(8,128)} collective-permute-done((f32[136,256]{1,0:T(8,128)}, f32[136,256]{1,0:T(8,128)}, u32[]{:S(2)}, u32[]{:S(2)}) %collective-permute-start.43) | collective-permute-done | bytes 139296 | tf_op jit(solution)/shard_map/ppermute | solution.py:427
  204.8 2.1 copy-done.10
  206.9 1.1 copy-done.24
  208.0 1.1 copy-done.26
  209.1 1.1 copy-done.28
  210.2 1.1 copy-done.30
  211.3 1.1 copy-done.32
  212.4 1.1 copy-done.34
  214.5 6.7 %shard_map.128.refs_1_ = bf16[768,1024]{1,0:T(8,128)(2,1)S(1)} custom-call(s32[32]{0:T(128)S(1)} %get-tuple-element.76.refs_0_, bf16[320,1024]{1,0:T(8,128)(2,1)S(1)} %pad_maximum_fusion.7.refs_1_, bf16[320,1024]{1,0:T(8,128)(2,1)S(1)} %copy-done.30, bf16[320,1024]{1,0:T(8,128)(2,1)S(1)} %copy-done.28, bf16[320,1024]{1,0:T(8,128)(2,1)S(1)} %copy-done.26, ...), custom_call_target="tpu_custom_call" | custom-call | flops 4026531840 | bytes 16000000 | tf_op jit(solution)/shard_map/pallas_call | solution.py:302
  221.2 6.2 %inner.2.refs_2_ = f32[768,1024]{1,0:T(8,128)S(1)} custom-call(bf16[768,1280]{1,0:T(8,128)(2,1)S(1)} %get-tuple-element.12.x_ref.bc_ref.refs_6_, bf16[768,1280]{1,0:T(8,128)(2,1)S(1)} %get-tuple-element.12.x_ref.bc_ref.refs_6_, f32[768,128]{1,0:T(8,128)S(1)} %get-tuple-element.13.cum_ref.refs_7_, f32[768,128]{1,0:T(8,128)S(1)} %get-tuple-element.14.step_ref, ...), custom_call_target="tpu_custom_call" | custom-call | flops 1207959552 | bytes 8000000 | tf_op jit(solution)/shard_map/inner/pallas_call | solution.py:362
  233.4 1.3 collective-permute-start.45
  235.6 1.9 collective-permute-start.44
  237.6 1.2 copy-done.14
  238.8 1.2 copy-done.16
  240.0 1.2 copy-done.18
  241.2 13.6 %shard_map.130.x_ref = bf16[768,1536]{1,0:T(8,128)(2,1)S(1)} custom-call(s32[32]{0:T(128)S(1)} %get-tuple-element.75.refs_0_, s32[1]{0:T(128)} %bitcast.refs_1_.blocks_ref, bf16[320,1536]{1,0:T(8,128)(2,1)} %pad_maximum_fusion.1.refs_2_, bf16[320,1536]{1,0:T(8,128)(2,1)} %collective-permute-done.34.refs_3_, ...), custom_call_target="tpu_custom_call" | custom-call | flops 6039797760 | bytes 16000000 | tf_op jit(solution)/shard_map/pallas_call | solution.py:302
  254.8 3.4 %summary.3 = (f32[3,128,1536]{2,1,0:T(8,128)S(1)}, f32[4,136,384]{2,1,0:T(8,128)S(1)}) custom-call(bf16[768,1536]{1,0:T(8,128)(2,1)S(1)} %shard_map.130.x_ref, bf16[768,1280]{1,0:T(8,128)(2,1)S(1)} %get-tuple-element.12.x_ref.bc_ref.refs_6_, f32[768,128]{1,0:T(8,128)S(1)} %get-tuple-element.13.cum_ref.refs_7_, f32[768,128]{1,0:T(8,128)S(1)} %get-tuple-element.14.step_ref), custom_call_target="tpu_custom_call" | custom-call | flops 603979776 | bytes 8000000 | tf_op jit(solution)/shard_map/summary/pallas_call | solution.py:344
  262.7 1.1 collective-permute-start.51
  263.9 2.0 collective-permute-start.50
  266.3 9.0 %shard_map.127.refs_0_ = bf16[768,1536]{1,0:T(8,128)(2,1)S(1)} custom-call(s32[32]{0:T(128)S(1)} %get-tuple-element.75.refs_0_, bf16[320,1536]{1,0:T(8,128)(2,1)} %pad_maximum_fusion.refs_1_, bf16[320,1536]{1,0:T(8,128)(2,1)} %collective-permute-done.3.refs_2_, bf16[320,1536]{1,0:T(8,128)(2,1)S(1)} %collective-permute-done.4.refs_3_, ...), custom_call_target="tpu_custom_call" | custom-call | flops 6039797760 | bytes 16000000 | tf_op jit(solution)/shard_map/pallas_call | solution.py:302
  275.4 1.4 copy-done.1
  277.8 2.0 collective-permute-start.47
  279.8 1.7 copy-done.4
  281.5 9.2 %inner.3.refs_3_ = f32[768,1536]{1,0:T(8,128)S(1)} custom-call(bf16[768,1536]{1,0:T(8,128)(2,1)S(1)} %shard_map.130.x_ref, bf16[768,1280]{1,0:T(8,128)(2,1)S(1)} %get-tuple-element.12.x_ref.bc_ref.refs_6_, f32[768,128]{1,0:T(8,128)S(1)} %get-tuple-element.13.cum_ref.refs_7_, f32[768,128]{1,0:T(8,128)S(1)} %get-tuple-element.14.step_ref, ...), custom_call_target="tpu_custom_call" | custom-call | flops 1811939328 | bytes 8000000 | tf_op jit(solution)/shard_map/inner/pallas_call | solution.py:362
  290.7 2.2 copy-done
  293.9 1.3 collective-permute-start.54
  295.2 1.9 collective-permute-start.53
  297.1 13.3 %collective-permute-done.54 = f32[136,384]{1,0:T(8,128)S(1)} collective-permute-done((f32[136,384]{1,0:T(8,128)S(1)}, f32[136,384]{1,0:T(8,128)S(1)}, u32[]{:S(2)}, u32[]{:S(2)}) %collective-permute-start.54) | collective-permute-done | bytes 208928 | tf_op jit(solution)/shard_map/ppermute | solution.py:427
  310.5 3.9 %collective-permute-done.53 = f32[136,384]{1,0:T(8,128)S(1)} collective-permute-done((f32[136,384]{1,0:T(8,128)S(1)}, f32[136,384]{1,0:T(8,128)S(1)}, u32[]{:S(2)}, u32[]{:S(2)}) %collective-permute-start.53) | collective-permute-done | bytes 208928 | tf_op jit(solution)/shard_map/ppermute | solution.py:427
  314.6 1.1 collective-permute-start.58
  316.8 1.4 collective-permute-start.56
  318.3 3.9 %collective-permute-done.58 = f32[128,384]{1,0:T(8,128)S(1)} collective-permute-done((f32[128,384]{1,0:T(8,128)S(1)}, f32[128,384]{1,0:T(8,128)S(1)}, u32[]{:S(2)}, u32[]{:S(2)}) %collective-permute-start.58) | collective-permute-done | bytes 196640 | tf_op jit(solution)/shard_map/ppermute | solution.py:427
  322.2 2.0 collective-permute-done.57
  324.4 1.5 copy-done.2
  325.9 8.4 %final.1 = bf16[768,2560]{1,0:T(8,128)(2,1)} custom-call(s32[1]{0:T(128)} %bitcast.refs_1_.blocks_ref, bf16[768,1536]{1,0:T(8,128)(2,1)S(1)} %copy-done.2, bf16[768,1024]{1,0:T(8,128)(2,1)S(1)} %shard_map.128.refs_1_, f32[768,1024]{1,0:T(8,128)S(1)} %inner.2.refs_2_, f32[768,1536]{1,0:T(8,128)} %copy-done, f32[128,1024]{1,0:T(8,128)S(1)} %pad_maximum_fusion.11.refs_4_, ...), custom_call_target="tpu_custom_call" | custom-call | flops 2013265920 | bytes 16000000 | tf_op jit(solution)/shard_map/final/pallas_call | solution.py:395
  (218 shorter events, 38.5 us)
Async XLA Ops:
  1.0 46.7 %collective-permute-start.11 = (bf16[80,1024]{1,0:T(8,128)(2,1)S(1)}, bf16[80,1024]{1,0:T(8,128)(2,1)S(1)}, u32[]{:S(2)}, u32[]{:S(2)}) collective-permute-start(bf16[80,1024]{1,0:T(8,128)(2,1)S(1)} %get-tuple-element.40), channel_id=1, source_target_pairs={{0,4},{1,3},{2,6},{3,1},{4,0},{5,7},{6,2},{7,5},{8,12},{9,11},{10,... | collective-permute-start | bytes 491528 | tf_op jit(solution)/shard_map/ppermute | solution.py:427
  2.6 35.1 %collective-permute-start.10 = (bf16[80,1024]{1,0:T(8,128)(2,1)S(1)}, bf16[80,1024]{1,0:T(8,128)(2,1)S(1)}, u32[]{:S(2)}, u32[]{:S(2)}) collective-permute-start(bf16[80,1024]{1,0:T(8,128)(2,1)S(1)} %get-tuple-element.40), channel_id=1, source_target_pairs={{0,2},{1,5},{2,0},{3,7},{4,6},{5,1},{6,4},{7,3},{8,10},{9,13},{10,... | collective-permute-start | bytes 491528 | tf_op jit(solution)/shard_map/ppermute | solution.py:427
  5.0 14.4 %collective-permute-start.22 = (bf16[80,1408]{1,0:T(8,128)(2,1)S(1)}, bf16[80,1408]{1,0:T(8,128)(2,1)S(1)}, u32[]{:S(2)}, u32[]{:S(2)}) collective-permute-start(bf16[80,1408]{1,0:T(8,128)(2,1)S(1)} %pad_maximum_fusion.12), channel_id=1, source_target_pairs={{0,24},{1,25},{2,26},{3,27},{4,28},{5,29},{6,30},{7,31},{8,0},{9,1... | collective-permute-start | bytes 675848 | tf_op jit(solution)/shard_map/ppermute | solution.py:427
  5.5 20.3 %collective-permute-start.21 = (bf16[80,1408]{1,0:T(8,128)(2,1)S(1)}, bf16[80,1408]{1,0:T(8,128)(2,1)S(1)}, u32[]{:S(2)}, u32[]{:S(2)}) collective-permute-start(bf16[80,1408]{1,0:T(8,128)(2,1)S(1)} %pad_maximum_fusion.12), channel_id=1, source_target_pairs={{0,16},{1,17},{2,18},{3,19},{4,20},{5,21},{6,22},{7,23},{8,24},{9,... | collective-permute-start | bytes 675848 | tf_op jit(solution)/shard_map/ppermute | solution.py:427
  9.0 23.7 %collective-permute-start.20 = (bf16[80,1408]{1,0:T(8,128)(2,1)S(1)}, bf16[80,1408]{1,0:T(8,128)(2,1)S(1)}, u32[]{:S(2)}, u32[]{:S(2)}) collective-permute-start(bf16[80,1408]{1,0:T(8,128)(2,1)S(1)} %pad_maximum_fusion.12), channel_id=1, source_target_pairs={{0,8},{1,9},{2,10},{3,11},{4,12},{5,13},{6,14},{7,15},{8,16},{9,17... | collective-permute-start | bytes 675848 | tf_op jit(solution)/shard_map/ppermute | solution.py:427
  19.4 29.4 %collective-permute-start.33 = (bf16[80,1536]{1,0:T(8,128)(2,1)S(1)}, bf16[80,1536]{1,0:T(8,128)(2,1)S(1)}, u32[]{:S(2)}, u32[]{:S(2)}) collective-permute-start(bf16[80,1536]{1,0:T(8,128)(2,1)S(1)} %get-tuple-element.37), channel_id=1, source_target_pairs={{0,24},{1,25},{2,26},{3,27},{4,28},{5,29},{6,30},{7,31},{8,0},{9,1... | collective-permute-start | bytes 737288 | tf_op jit(solution)/shard_map/ppermute | solution.py:427
  32.8 105.6 %copy-start.49 = (f32[40]{0:T(128)S(1)}, f32[40]{0:T(128)}, u32[]{:S(2)}) copy-start(f32[40]{0:T(128)} %param.20) | copy-start | bytes 484
  32.8 105.6 %copy-start.50 = (f32[40]{0:T(128)S(1)}, f32[40]{0:T(128)}, u32[]{:S(2)}) copy-start(f32[40]{0:T(128)} %param.19) | copy-start | bytes 484
  32.8 105.6 %copy-start.51 = (f32[40]{0:T(128)S(1)}, f32[40]{0:T(128)}, u32[]{:S(2)}) copy-start(f32[40]{0:T(128)} %param.18) | copy-start | bytes 484
  32.9 126.0 %copy-start.46 = (f32[2816]{0:T(1024)S(1)}, f32[2816]{0:T(1024)}, u32[]{:S(2)}) copy-start(f32[2816]{0:T(1024)} %param.17) | copy-start | bytes 33796
  32.9 59.9 %collective-permute-start.23 = (bf16[320,1408]{1,0:T(8,128)(2,1)S(1)}, bf16[320,1408]{1,0:T(8,128)(2,1)S(1)}, u32[]{:S(2)}, u32[]{:S(2)}) collective-permute-start(bf16[320,1408]{1,0:T(8,128)(2,1)S(1)} %pad_maximum_fusion.2.refs_2_), channel_id=1, source_target_pairs={{0,2},{1,5},{2,0},{3,7},{4,6},{5,1},{6,4},{7,3},{8,10},{9,13},{10,... | collective-permute-start | bytes 2703368 | tf_op jit(solution)/shard_map/ppermute | solution.py:427
  34.4 13.4 %collective-permute-start.30 = (bf16[16,2560]{1,0:T(8,128)(2,1)S(1)}, bf16[16,2560]{1,0:T(8,128)(2,1)S(1)}, u32[]{:S(2)}, u32[]{:S(2)}) collective-permute-start(bf16[16,2560]{1,0:T(8,128)(2,1)S(1)} %dynamic-slice_bitcast_fusion.28), channel_id=1, source_target_pairs={{0,2},{1,3},{2,4},{3,5},{4,6},{5,7},{6,8},{7,9},{8,10},{9,11},{10,... | collective-permute-start | bytes 245768 | tf_op jit(solution)/shard_map/ppermute | solution.py:427
  37.8 12.0 %collective-permute-start.12 = (bf16[80,1024]{1,0:T(8,128)(2,1)S(1)}, bf16[80,1024]{1,0:T(8,128)(2,1)S(1)}, u32[]{:S(2)}, u32[]{:S(2)}) collective-permute-start(bf16[80,1024]{1,0:T(8,128)(2,1)S(1)} %collective-permute-done.10), channel_id=1, source_target_pairs={{0,4},{1,3},{2,6},{3,1},{4,0},{5,7},{6,2},{7,5},{8,12},{9,11},{10,... | collective-permute-start | bytes 491528 | tf_op jit(solution)/shard_map/ppermute | solution.py:427
  47.7 16.9 %collective-permute-start.32 = (bf16[80,1536]{1,0:T(8,128)(2,1)S(1)}, bf16[80,1536]{1,0:T(8,128)(2,1)S(1)}, u32[]{:S(2)}, u32[]{:S(2)}) collective-permute-start(bf16[80,1536]{1,0:T(8,128)(2,1)S(1)} %get-tuple-element.37), channel_id=1, source_target_pairs={{0,16},{1,17},{2,18},{3,19},{4,20},{5,21},{6,22},{7,23},{8,24},{9,... | collective-permute-start | bytes 737288 | tf_op jit(solution)/shard_map/ppermute | solution.py:427
  47.7 24.3 %collective-permute-start.31 = (bf16[80,1536]{1,0:T(8,128)(2,1)S(1)}, bf16[80,1536]{1,0:T(8,128)(2,1)S(1)}, u32[]{:S(2)}, u32[]{:S(2)}) collective-permute-start(bf16[80,1536]{1,0:T(8,128)(2,1)S(1)} %get-tuple-element.37), channel_id=1, source_target_pairs={{0,8},{1,9},{2,10},{3,11},{4,12},{5,13},{6,14},{7,15},{8,16},{9,17... | collective-permute-start | bytes 737288 | tf_op jit(solution)/shard_map/ppermute | solution.py:427
  48.7 23.3 %collective-permute-start.2 = (bf16[80,1536]{1,0:T(8,128)(2,1)S(1)}, bf16[80,1536]{1,0:T(8,128)(2,1)S(1)}, u32[]{:S(2)}, u32[]{:S(2)}) collective-permute-start(bf16[80,1536]{1,0:T(8,128)(2,1)S(1)} %get-tuple-element.38), channel_id=1, source_target_pairs={{0,24},{1,25},{2,26},{3,27},{4,28},{5,29},{6,30},{7,31},{8,0},{9,1... | collective-permute-start | bytes 737288 | tf_op jit(solution)/shard_map/ppermute | solution.py:427
  49.8 25.3 %collective-permute-start.1 = (bf16[80,1536]{1,0:T(8,128)(2,1)S(1)}, bf16[80,1536]{1,0:T(8,128)(2,1)S(1)}, u32[]{:S(2)}, u32[]{:S(2)}) collective-permute-start(bf16[80,1536]{1,0:T(8,128)(2,1)S(1)} %get-tuple-element.38), channel_id=1, source_target_pairs={{0,16},{1,17},{2,18},{3,19},{4,20},{5,21},{6,22},{7,23},{8,24},{9,... | collective-permute-start | bytes 737288 | tf_op jit(solution)/shard_map/ppermute | solution.py:427
  64.6 28.6 %collective-permute-start.16 = (bf16[320,1024]{1,0:T(8,128)(2,1)S(1)}, bf16[320,1024]{1,0:T(8,128)(2,1)S(1)}, u32[]{:S(2)}, u32[]{:S(2)}) collective-permute-start(bf16[320,1024]{1,0:T(8,128)(2,1)S(1)} %pad_maximum_fusion.7.refs_1_), channel_id=1, source_target_pairs={{0,1},{1,0},{2,3},{3,2},{4,5},{5,4},{6,7},{7,6},{8,9},{9,8},{10,11... | collective-permute-start | bytes 1966088 | tf_op jit(solution)/shard_map/ppermute | solution.py:427
  72.1 22.1 %collective-permute-start.15 = (bf16[320,1024]{1,0:T(8,128)(2,1)S(1)}, bf16[320,1024]{1,0:T(8,128)(2,1)S(1)}, u32[]{:S(2)}, u32[]{:S(2)}) collective-permute-start(bf16[320,1024]{1,0:T(8,128)(2,1)S(1)} %pad_maximum_fusion.7.refs_1_), channel_id=1, source_target_pairs={{0,24},{1,25},{2,26},{3,27},{4,28},{5,29},{6,30},{7,31},{8,0},{9,1... | collective-permute-start | bytes 1966088 | tf_op jit(solution)/shard_map/ppermute | solution.py:427
  72.1 20.7 %collective-permute-start = (bf16[80,1536]{1,0:T(8,128)(2,1)S(1)}, bf16[80,1536]{1,0:T(8,128)(2,1)S(1)}, u32[]{:S(2)}, u32[]{:S(2)}) collective-permute-start(bf16[80,1536]{1,0:T(8,128)(2,1)S(1)} %get-tuple-element.38), channel_id=1, source_target_pairs={{0,8},{1,9},{2,10},{3,11},{4,12},{5,13},{6,14},{7,15},{8,16},{9,17... | collective-permute-start | bytes 737288 | tf_op jit(solution)/shard_map/ppermute | solution.py:427
  75.1 58.8 %collective-permute-start.24 = (bf16[320,1408]{1,0:T(8,128)(2,1)S(1)}, bf16[320,1408]{1,0:T(8,128)(2,1)}, u32[]{:S(2)}, u32[]{:S(2)}) collective-permute-start(bf16[320,1408]{1,0:T(8,128)(2,1)S(1)} %pad_maximum_fusion.2.refs_2_), channel_id=1, source_target_pairs={{0,4},{1,3},{2,6},{3,1},{4,0},{5,7},{6,2},{7,5},{8,12},{9,11},{10,... | collective-permute-start | bytes 2703368 | tf_op jit(solution)/shard_map/ppermute | solution.py:427
  92.8 41.1 %collective-permute-start.14 = (bf16[320,1024]{1,0:T(8,128)(2,1)S(1)}, bf16[320,1024]{1,0:T(8,128)(2,1)S(1)}, u32[]{:S(2)}, u32[]{:S(2)}) collective-permute-start(bf16[320,1024]{1,0:T(8,128)(2,1)S(1)} %pad_maximum_fusion.7.refs_1_), channel_id=1, source_target_pairs={{0,16},{1,17},{2,18},{3,19},{4,20},{5,21},{6,22},{7,23},{8,24},{9,... | collective-permute-start | bytes 1966088 | tf_op jit(solution)/shard_map/ppermute | solution.py:427
  92.8 68.5 %copy-start.19 = (bf16[320,1408]{1,0:T(8,128)(2,1)}, bf16[320,1408]{1,0:T(8,128)(2,1)S(1)}, u32[]{:S(2)}) copy-start(bf16[320,1408]{1,0:T(8,128)(2,1)S(1)} %collective-permute-done.23.refs_3_) | copy-start | bytes 2703364
  92.8 42.4 %collective-permute-start.25 = (bf16[320,1408]{1,0:T(8,128)(2,1)S(1)}, bf16[320,1408]{1,0:T(8,128)(2,1)}, u32[]{:S(2)}, u32[]{:S(2)}) collective-permute-start(bf16[320,1408]{1,0:T(8,128)(2,1)S(1)} %collective-permute-done.23.refs_3_), channel_id=1, source_target_pairs={{0,4},{1,3},{2,6},{3,1},{4,0},{5,7},{6,2},{7,5},{8,12},{9,11},{10,... | collective-permute-start | bytes 2703368 | tf_op jit(solution)/shard_map/ppermute | solution.py:427
  94.1 41.6 %collective-permute-start.26 = (bf16[320,1408]{1,0:T(8,128)(2,1)S(1)}, bf16[320,1408]{1,0:T(8,128)(2,1)S(1)}, u32[]{:S(2)}, u32[]{:S(2)}) collective-permute-start(bf16[320,1408]{1,0:T(8,128)(2,1)S(1)} %pad_maximum_fusion.2.refs_2_), channel_id=1, source_target_pairs={{0,1},{1,0},{2,3},{3,2},{4,5},{5,4},{6,7},{7,6},{8,9},{9,8},{10,11... | collective-permute-start | bytes 2703368 | tf_op jit(solution)/shard_map/ppermute | solution.py:427
  95.0 40.2 %collective-permute-start.13 = (bf16[320,1024]{1,0:T(8,128)(2,1)S(1)}, bf16[320,1024]{1,0:T(8,128)(2,1)S(1)}, u32[]{:S(2)}, u32[]{:S(2)}) collective-permute-start(bf16[320,1024]{1,0:T(8,128)(2,1)S(1)} %pad_maximum_fusion.7.refs_1_), channel_id=1, source_target_pairs={{0,8},{1,9},{2,10},{3,11},{4,12},{5,13},{6,14},{7,15},{8,16},{9,17... | collective-permute-start | bytes 1966088 | tf_op jit(solution)/shard_map/ppermute | solution.py:427
  133.9 23.1 %collective-permute-start.34 = (bf16[320,1536]{1,0:T(8,128)(2,1)}, bf16[320,1536]{1,0:T(8,128)(2,1)}, u32[]{:S(2)}, u32[]{:S(2)}) collective-permute-start(bf16[320,1536]{1,0:T(8,128)(2,1)} %pad_maximum_fusion.1.refs_2_), channel_id=1, source_target_pairs={{0,2},{1,5},{2,0},{3,7},{4,6},{5,1},{6,4},{7,3},{8,10},{9,13},{10,... | collective-permute-start | bytes 2949128 | tf_op jit(solution)/shard_map/ppermute | solution.py:427
  134.0 24.9 %collective-permute-start.28 = (bf16[320,1408]{1,0:T(8,128)(2,1)}, bf16[320,1408]{1,0:T(8,128)(2,1)}, u32[]{:S(2)}, u32[]{:S(2)}) collective-permute-start(bf16[320,1408]{1,0:T(8,128)(2,1)} %collective-permute-done.24.refs_4_), channel_id=1, source_target_pairs={{0,1},{1,0},{2,3},{3,2},{4,5},{5,4},{6,7},{7,6},{8,9},{9,8},{10,11... | collective-permute-start | bytes 2703368 | tf_op jit(solution)/shard_map/ppermute | solution.py:427
  135.2 26.1 %collective-permute-start.27 = (bf16[320,1408]{1,0:T(8,128)(2,1)S(1)}, bf16[320,1408]{1,0:T(8,128)(2,1)}, u32[]{:S(2)}, u32[]{:S(2)}) collective-permute-start(bf16[320,1408]{1,0:T(8,128)(2,1)S(1)} %collective-permute-done.23.refs_3_), channel_id=1, source_target_pairs={{0,1},{1,0},{2,3},{3,2},{4,5},{5,4},{6,7},{7,6},{8,9},{9,8},{10,11... | collective-permute-start | bytes 2703368 | tf_op jit(solution)/shard_map/ppermute | solution.py:427
  135.2 26.4 %collective-permute-start.29 = (bf16[320,1408]{1,0:T(8,128)(2,1)}, bf16[320,1408]{1,0:T(8,128)(2,1)}, u32[]{:S(2)}, u32[]{:S(2)}) collective-permute-start(bf16[320,1408]{1,0:T(8,128)(2,1)} %collective-permute-done.25.refs_5_), channel_id=1, source_target_pairs={{0,1},{1,0},{2,3},{3,2},{4,5},{5,4},{6,7},{7,6},{8,9},{9,8},{10,11... | collective-permute-start | bytes 2703368 | tf_op jit(solution)/shard_map/ppermute | solution.py:427
  136.7 47.3 %collective-permute-start.35 = (bf16[320,1536]{1,0:T(8,128)(2,1)}, bf16[320,1536]{1,0:T(8,128)(2,1)}, u32[]{:S(2)}, u32[]{:S(2)}) collective-permute-start(bf16[320,1536]{1,0:T(8,128)(2,1)} %pad_maximum_fusion.1.refs_2_), channel_id=1, source_target_pairs={{0,4},{1,3},{2,6},{3,1},{4,0},{5,7},{6,2},{7,5},{8,12},{9,11},{10,... | collective-permute-start | bytes 2949128 | tf_op jit(solution)/shard_map/ppermute | solution.py:427
  157.0 33.4 %collective-permute-start.36 = (bf16[320,1536]{1,0:T(8,128)(2,1)}, bf16[320,1536]{1,0:T(8,128)(2,1)}, u32[]{:S(2)}, u32[]{:S(2)}) collective-permute-start(bf16[320,1536]{1,0:T(8,128)(2,1)} %collective-permute-done.34.refs_3_), channel_id=1, source_target_pairs={{0,4},{1,3},{2,6},{3,1},{4,0},{5,7},{6,2},{7,5},{8,12},{9,11},{10,... | collective-permute-start | bytes 2949128 | tf_op jit(solution)/shard_map/ppermute | solution.py:427
  158.9 25.5 %collective-permute-start.19 = (bf16[320,1024]{1,0:T(8,128)(2,1)}, bf16[320,1024]{1,0:T(8,128)(2,1)S(1)}, u32[]{:S(2)}, u32[]{:S(2)}) collective-permute-start(bf16[320,1024]{1,0:T(8,128)(2,1)} %copy-done.25), channel_id=1, source_target_pairs={{0,1},{1,0},{2,3},{3,2},{4,5},{5,4},{6,7},{7,6},{8,9},{9,8},{10,11... | collective-permute-start | bytes 1966088 | tf_op jit(solution)/shard_map/ppermute | solution.py:427
  161.3 24.1 %collective-permute-start.18 = (bf16[320,1024]{1,0:T(8,128)(2,1)}, bf16[320,1024]{1,0:T(8,128)(2,1)S(1)}, u32[]{:S(2)}, u32[]{:S(2)}) collective-permute-start(bf16[320,1024]{1,0:T(8,128)(2,1)} %copy-done.27), channel_id=1, source_target_pairs={{0,1},{1,0},{2,3},{3,2},{4,5},{5,4},{6,7},{7,6},{8,9},{9,8},{10,11... | collective-permute-start | bytes 1966088 | tf_op jit(solution)/shard_map/ppermute | solution.py:427
  161.7 26.8 %collective-permute-start.17 = (bf16[320,1024]{1,0:T(8,128)(2,1)}, bf16[320,1024]{1,0:T(8,128)(2,1)S(1)}, u32[]{:S(2)}, u32[]{:S(2)}) collective-permute-start(bf16[320,1024]{1,0:T(8,128)(2,1)} %copy-done.29), channel_id=1, source_target_pairs={{0,1},{1,0},{2,3},{3,2},{4,5},{5,4},{6,7},{7,6},{8,9},{9,8},{10,11... | collective-permute-start | bytes 1966088 | tf_op jit(solution)/shard_map/ppermute | solution.py:427
  184.0 45.6 %collective-permute-start.37 = (bf16[320,1536]{1,0:T(8,128)(2,1)}, bf16[320,1536]{1,0:T(8,128)(2,1)}, u32[]{:S(2)}, u32[]{:S(2)}) collective-permute-start(bf16[320,1536]{1,0:T(8,128)(2,1)} %pad_maximum_fusion.1.refs_2_), channel_id=1, source_target_pairs={{0,1},{1,0},{2,3},{3,2},{4,5},{5,4},{6,7},{7,6},{8,9},{9,8},{10,11... | collective-permute-start | bytes 2949128 | tf_op jit(solution)/shard_map/ppermute | solution.py:427
  184.4 44.2 %collective-permute-start.3 = (bf16[320,1536]{1,0:T(8,128)(2,1)}, bf16[320,1536]{1,0:T(8,128)(2,1)}, u32[]{:S(2)}, u32[]{:S(2)}) collective-permute-start(bf16[320,1536]{1,0:T(8,128)(2,1)} %pad_maximum_fusion.refs_1_), channel_id=1, source_target_pairs={{0,2},{1,5},{2,0},{3,7},{4,6},{5,1},{6,4},{7,3},{8,10},{9,13},{10,... | collective-permute-start | bytes 2949128 | tf_op jit(solution)/shard_map/ppermute | solution.py:427
  186.3 17.5 %collective-permute-start.43 = (f32[136,256]{1,0:T(8,128)}, f32[136,256]{1,0:T(8,128)}, u32[]{:S(2)}, u32[]{:S(2)}) collective-permute-start(f32[136,256]{1,0:T(8,128)} %get-tuple-element.58), channel_id=1, source_target_pairs={{0,6},{1,7},{2,4},{3,5},{4,2},{5,3},{6,0},{7,1},{8,14},{9,15},{10,... | collective-permute-start | bytes 417800 | tf_op jit(solution)/shard_map/ppermute | solution.py:427
  189.3 14.4 %collective-permute-start.42 = (f32[136,256]{1,0:T(8,128)}, f32[136,256]{1,0:T(8,128)}, u32[]{:S(2)}, u32[]{:S(2)}) collective-permute-start(f32[136,256]{1,0:T(8,128)} %get-tuple-element.59), channel_id=1, source_target_pairs={{0,4},{1,5},{2,6},{3,7},{4,0},{5,1},{6,2},{7,3},{8,12},{9,13},{10,... | collective-permute-start | bytes 417800 | tf_op jit(solution)/shard_map/ppermute | solution.py:427
  190.4 14.4 %collective-permute-start.41 = (f32[136,256]{1,0:T(8,128)}, f32[136,256]{1,0:T(8,128)}, u32[]{:S(2)}, u32[]{:S(2)}) collective-permute-start(f32[136,256]{1,0:T(8,128)} %get-tuple-element.60), channel_id=1, source_target_pairs={{0,2},{1,3},{2,0},{3,1},{4,6},{5,7},{6,4},{7,5},{8,10},{9,11},{10,... | collective-permute-start | bytes 417800 | tf_op jit(solution)/shard_map/ppermute | solution.py:427
  203.7 28.7 %collective-permute-start.38 = (bf16[320,1536]{1,0:T(8,128)(2,1)}, bf16[320,1536]{1,0:T(8,128)(2,1)S(1)}, u32[]{:S(2)}, u32[]{:S(2)}) collective-permute-start(bf16[320,1536]{1,0:T(8,128)(2,1)} %collective-permute-done.34.refs_3_), channel_id=1, source_target_pairs={{0,1},{1,0},{2,3},{3,2},{4,5},{5,4},{6,7},{7,6},{8,9},{9,8},{10,11... | collective-permute-start | bytes 2949128 | tf_op jit(solution)/shard_map/ppermute | solution.py:427
  203.8 27.0 %collective-permute-start.39 = (bf16[320,1536]{1,0:T(8,128)(2,1)}, bf16[320,1536]{1,0:T(8,128)(2,1)S(1)}, u32[]{:S(2)}, u32[]{:S(2)}) collective-permute-start(bf16[320,1536]{1,0:T(8,128)(2,1)} %collective-permute-done.35.refs_4_), channel_id=1, source_target_pairs={{0,1},{1,0},{2,3},{3,2},{4,5},{5,4},{6,7},{7,6},{8,9},{9,8},{10,11... | collective-permute-start | bytes 2949128 | tf_op jit(solution)/shard_map/ppermute | solution.py:427
  204.8 29.9 %collective-permute-start.40 = (bf16[320,1536]{1,0:T(8,128)(2,1)}, bf16[320,1536]{1,0:T(8,128)(2,1)S(1)}, u32[]{:S(2)}, u32[]{:S(2)}) collective-permute-start(bf16[320,1536]{1,0:T(8,128)(2,1)} %collective-permute-done.36.refs_5_), channel_id=1, source_target_pairs={{0,1},{1,0},{2,3},{3,2},{4,5},{5,4},{6,7},{7,6},{8,9},{9,8},{10,11... | collective-permute-start | bytes 2949128 | tf_op jit(solution)/shard_map/ppermute | solution.py:427
  228.5 29.7 %collective-permute-start.4 = (bf16[320,1536]{1,0:T(8,128)(2,1)}, bf16[320,1536]{1,0:T(8,128)(2,1)S(1)}, u32[]{:S(2)}, u32[]{:S(2)}) collective-permute-start(bf16[320,1536]{1,0:T(8,128)(2,1)} %pad_maximum_fusion.refs_1_), channel_id=1, source_target_pairs={{0,4},{1,3},{2,6},{3,1},{4,0},{5,7},{6,2},{7,5},{8,12},{9,11},{10,... | collective-permute-start | bytes 2949128 | tf_op jit(solution)/shard_map/ppermute | solution.py:427
  229.6 28.7 %collective-permute-start.5 = (bf16[320,1536]{1,0:T(8,128)(2,1)}, bf16[320,1536]{1,0:T(8,128)(2,1)S(1)}, u32[]{:S(2)}, u32[]{:S(2)}) collective-permute-start(bf16[320,1536]{1,0:T(8,128)(2,1)} %collective-permute-done.3.refs_2_), channel_id=1, source_target_pairs={{0,4},{1,3},{2,6},{3,1},{4,0},{5,7},{6,2},{7,5},{8,12},{9,11},{10,... | collective-permute-start | bytes 2949128 | tf_op jit(solution)/shard_map/ppermute | solution.py:427
  231.7 29.4 %collective-permute-start.46 = (f32[136,256]{1,0:T(8,128)S(1)}, f32[136,256]{1,0:T(8,128)S(1)}, u32[]{:S(2)}, u32[]{:S(2)}) collective-permute-start(f32[136,256]{1,0:T(8,128)S(1)} %pad_maximum_fusion.14), channel_id=1, source_target_pairs={{0,24},{1,25},{2,26},{3,27},{4,28},{5,29},{6,30},{7,31}} | collective-permute-start | bytes 417800 | tf_op jit(solution)/shard_map/ppermute | solution.py:427
  233.4 25.4 %collective-permute-start.45 = (f32[136,256]{1,0:T(8,128)S(1)}, f32[136,256]{1,0:T(8,128)}, u32[]{:S(2)}, u32[]{:S(2)}) collective-permute-start(f32[136,256]{1,0:T(8,128)S(1)} %pad_maximum_fusion.14), channel_id=1, source_target_pairs={{0,16},{1,17},{2,18},{3,19},{4,20},{5,21},{6,22},{7,23},{8,24},{9,... | collective-permute-start | bytes 417800 | tf_op jit(solution)/shard_map/ppermute | solution.py:427
  235.6 23.2 %collective-permute-start.44 = (f32[136,256]{1,0:T(8,128)S(1)}, f32[136,256]{1,0:T(8,128)}, u32[]{:S(2)}, u32[]{:S(2)}) collective-permute-start(f32[136,256]{1,0:T(8,128)S(1)} %pad_maximum_fusion.14), channel_id=1, source_target_pairs={{0,8},{1,9},{2,10},{3,11},{4,12},{5,13},{6,14},{7,15},{8,16},{9,17... | collective-permute-start | bytes 417800 | tf_op jit(solution)/shard_map/ppermute | solution.py:427
  258.2 4.4 %collective-permute-start.6 = (bf16[320,1536]{1,0:T(8,128)(2,1)}, bf16[320,1536]{1,0:T(8,128)(2,1)S(1)}, u32[]{:S(2)}, u32[]{:S(2)}) collective-permute-start(bf16[320,1536]{1,0:T(8,128)(2,1)} %pad_maximum_fusion.refs_1_), channel_id=1, source_target_pairs={{0,1},{1,0},{2,3},{3,2},{4,5},{5,4},{6,7},{7,6},{8,9},{9,8},{10,11... | collective-permute-start | bytes 2949128 | tf_op jit(solution)/shard_map/ppermute | solution.py:427
  258.3 7.6 %collective-permute-start.7 = (bf16[320,1536]{1,0:T(8,128)(2,1)}, bf16[320,1536]{1,0:T(8,128)(2,1)S(1)}, u32[]{:S(2)}, u32[]{:S(2)}) collective-permute-start(bf16[320,1536]{1,0:T(8,128)(2,1)} %collective-permute-done.3.refs_2_), channel_id=1, source_target_pairs={{0,1},{1,0},{2,3},{3,2},{4,5},{5,4},{6,7},{7,6},{8,9},{9,8},{10,11... | collective-permute-start | bytes 2949128 | tf_op jit(solution)/shard_map/ppermute | solution.py:427
  258.8 5.1 %collective-permute-start.8 = (bf16[320,1536]{1,0:T(8,128)(2,1)S(1)}, bf16[320,1536]{1,0:T(8,128)(2,1)S(1)}, u32[]{:S(2)}, u32[]{:S(2)}) collective-permute-start(bf16[320,1536]{1,0:T(8,128)(2,1)S(1)} %collective-permute-done.4.refs_3_), channel_id=1, source_target_pairs={{0,1},{1,0},{2,3},{3,2},{4,5},{5,4},{6,7},{7,6},{8,9},{9,8},{10,11... | collective-permute-start | bytes 2949128 | tf_op jit(solution)/shard_map/ppermute | solution.py:427
  258.9 7.5 %collective-permute-start.9 = (bf16[320,1536]{1,0:T(8,128)(2,1)S(1)}, bf16[320,1536]{1,0:T(8,128)(2,1)S(1)}, u32[]{:S(2)}, u32[]{:S(2)}) collective-permute-start(bf16[320,1536]{1,0:T(8,128)(2,1)S(1)} %collective-permute-done.5.refs_4_), channel_id=1, source_target_pairs={{0,1},{1,0},{2,3},{3,2},{4,5},{5,4},{6,7},{7,6},{8,9},{9,8},{10,11... | collective-permute-start | bytes 2949128 | tf_op jit(solution)/shard_map/ppermute | solution.py:427
  261.1 31.8 %collective-permute-start.52 = (f32[136,384]{1,0:T(8,128)S(1)}, f32[136,384]{1,0:T(8,128)S(1)}, u32[]{:S(2)}, u32[]{:S(2)}) collective-permute-start(f32[136,384]{1,0:T(8,128)S(1)} %get-tuple-element.42), channel_id=1, source_target_pairs={{0,6},{1,7},{2,4},{3,5},{4,2},{5,3},{6,0},{7,1},{8,14},{9,15},{10,... | collective-permute-start | bytes 626696 | tf_op jit(solution)/shard_map/ppermute | solution.py:427
  262.7 30.3 %collective-permute-start.51 = (f32[136,384]{1,0:T(8,128)S(1)}, f32[136,384]{1,0:T(8,128)S(1)}, u32[]{:S(2)}, u32[]{:S(2)}) collective-permute-start(f32[136,384]{1,0:T(8,128)S(1)} %get-tuple-element.43), channel_id=1, source_target_pairs={{0,4},{1,5},{2,6},{3,7},{4,0},{5,1},{6,2},{7,3},{8,12},{9,13},{10,... | collective-permute-start | bytes 626696 | tf_op jit(solution)/shard_map/ppermute | solution.py:427
  263.9 29.1 %collective-permute-start.50 = (f32[136,384]{1,0:T(8,128)S(1)}, f32[136,384]{1,0:T(8,128)S(1)}, u32[]{:S(2)}, u32[]{:S(2)}) collective-permute-start(f32[136,384]{1,0:T(8,128)S(1)} %get-tuple-element.44), channel_id=1, source_target_pairs={{0,2},{1,3},{2,0},{3,1},{4,6},{5,7},{6,4},{7,5},{8,10},{9,11},{10,... | collective-permute-start | bytes 626696 | tf_op jit(solution)/shard_map/ppermute | solution.py:427
  265.9 11.9 %collective-permute-start.49 = (f32[128,256]{1,0:T(8,128)S(1)}, f32[128,256]{1,0:T(8,128)S(1)}, u32[]{:S(2)}, u32[]{:S(2)}) collective-permute-start(f32[128,256]{1,0:T(8,128)S(1)} %get-tuple-element.66), channel_id=1, source_target_pairs={{0,6},{1,7},{2,4},{3,5},{4,2},{5,3},{6,0},{7,1},{8,14},{9,15},{10,... | collective-permute-start | bytes 393224 | tf_op jit(solution)/shard_map/ppermute | solution.py:427
  276.8 16.1 %collective-permute-start.48 = (f32[128,256]{1,0:T(8,128)S(1)}, f32[128,256]{1,0:T(8,128)S(1)}, u32[]{:S(2)}, u32[]{:S(2)}) collective-permute-start(f32[128,256]{1,0:T(8,128)S(1)} %get-tuple-element.67), channel_id=1, source_target_pairs={{0,4},{1,5},{2,6},{3,7},{4,0},{5,1},{6,2},{7,3},{8,12},{9,13},{10,... | collective-permute-start | bytes 393224 | tf_op jit(solution)/shard_map/ppermute | solution.py:427
  277.8 15.0 %collective-permute-start.47 = (f32[128,256]{1,0:T(8,128)S(1)}, f32[128,256]{1,0:T(8,128)S(1)}, u32[]{:S(2)}, u32[]{:S(2)}) collective-permute-start(f32[128,256]{1,0:T(8,128)S(1)} %get-tuple-element.68), channel_id=1, source_target_pairs={{0,2},{1,3},{2,0},{3,1},{4,6},{5,7},{6,4},{7,5},{8,10},{9,11},{10,... | collective-permute-start | bytes 393224 | tf_op jit(solution)/shard_map/ppermute | solution.py:427
  293.2 17.3 %collective-permute-start.55 = (f32[136,384]{1,0:T(8,128)S(1)}, f32[136,384]{1,0:T(8,128)S(1)}, u32[]{:S(2)}, u32[]{:S(2)}) collective-permute-start(f32[136,384]{1,0:T(8,128)S(1)} %pad_maximum_fusion.13), channel_id=1, source_target_pairs={{0,24},{1,25},{2,26},{3,27},{4,28},{5,29},{6,30},{7,31}} | collective-permute-start | bytes 626696 | tf_op jit(solution)/shard_map/ppermute | solution.py:427
  293.9 16.6 %collective-permute-start.54 = (f32[136,384]{1,0:T(8,128)S(1)}, f32[136,384]{1,0:T(8,128)S(1)}, u32[]{:S(2)}, u32[]{:S(2)}) collective-permute-start(f32[136,384]{1,0:T(8,128)S(1)} %pad_maximum_fusion.13), channel_id=1, source_target_pairs={{0,16},{1,17},{2,18},{3,19},{4,20},{5,21},{6,22},{7,23},{8,24},{9,... | collective-permute-start | bytes 626696 | tf_op jit(solution)/shard_map/ppermute | solution.py:427
  295.2 19.2 %collective-permute-start.53 = (f32[136,384]{1,0:T(8,128)S(1)}, f32[136,384]{1,0:T(8,128)S(1)}, u32[]{:S(2)}, u32[]{:S(2)}) collective-permute-start(f32[136,384]{1,0:T(8,128)S(1)} %pad_maximum_fusion.13), channel_id=1, source_target_pairs={{0,8},{1,9},{2,10},{3,11},{4,12},{5,13},{6,14},{7,15},{8,16},{9,17... | collective-permute-start | bytes 626696 | tf_op jit(solution)/shard_map/ppermute | solution.py:427
  314.6 7.5 %collective-permute-start.58 = (f32[128,384]{1,0:T(8,128)S(1)}, f32[128,384]{1,0:T(8,128)S(1)}, u32[]{:S(2)}, u32[]{:S(2)}) collective-permute-start(f32[128,384]{1,0:T(8,128)S(1)} %get-tuple-element.50), channel_id=1, source_target_pairs={{0,6},{1,7},{2,4},{3,5},{4,2},{5,3},{6,0},{7,1},{8,14},{9,15},{10,... | collective-permute-start | bytes 589832 | tf_op jit(solution)/shard_map/ppermute | solution.py:427
  315.7 8.4 %collective-permute-start.57 = (f32[128,384]{1,0:T(8,128)S(1)}, f32[128,384]{1,0:T(8,128)S(1)}, u32[]{:S(2)}, u32[]{:S(2)}) collective-permute-start(f32[128,384]{1,0:T(8,128)S(1)} %get-tuple-element.51), channel_id=1, source_target_pairs={{0,4},{1,5},{2,6},{3,7},{4,0},{5,1},{6,2},{7,3},{8,12},{9,13},{10,... | collective-permute-start | bytes 589832 | tf_op jit(solution)/shard_map/ppermute | solution.py:427
  316.8 7.4 %collective-permute-start.56 = (f32[128,384]{1,0:T(8,128)S(1)}, f32[128,384]{1,0:T(8,128)S(1)}, u32[]{:S(2)}, u32[]{:S(2)}) collective-permute-start(f32[128,384]{1,0:T(8,128)S(1)} %get-tuple-element.52), channel_id=1, source_target_pairs={{0,2},{1,3},{2,0},{3,1},{4,6},{5,7},{6,4},{7,5},{8,10},{9,11},{10,... | collective-permute-start | bytes 589832 | tf_op jit(solution)/shard_map/ppermute | solution.py:427
  (47 other events, 284.7 us)
